TPU v7x, 32 devices: a whole 2x2x4 slice. The times are simulated.
32 devices in a mesh: bank: 8 (over y, x, core), zero: 4 (over z).
Axes of the slice: x: 2, y: 2, z: 4, core: 2. Of those that a mesh axis runs over, the one named last changes fastest.
Arguments:
- master_down: float32 [64, 1024, 2048], P('bank', None, 'zero'), may hold values from -0.25 to 0.25
- router_weight: float32 [2048, 64], P('zero', 'bank'), may hold values from -0.125 to 0.125
- router_gain: float32 [2048], P('zero'), may hold values from 0.25 to 1.75
Outputs:
- final_down: bfloat16 [64, 1024, 2048], P('bank')
- scale_down: float32 [64, 1024], P('bank')
- serve_router: bfloat16 [2048, 64], replicated
All inputs are finite; a program needn't handle non-finite values. Where the computation divides by a largest or mean magnitude, that divisor is 1e-20 or more.
Results may differ from a plain program's by a relative error of at most 0.001.
Values may be sent and summed in bfloat16 or wider, within the bound.
A program may use at most 128 MiB of HBM per device.

v0:
```python
import jax
import jax.numpy as jnp
from jax import lax
from jax.sharding import PartitionSpec as P


def per_device(master_down, router_weight, router_gain):
    scale_down = lax.pmax(jnp.max(jnp.abs(master_down), axis=2), "zero")
    narrow_down = (master_down / jnp.expand_dims(scale_down, 2)).astype(jnp.bfloat16)
    final_down = lax.all_gather(narrow_down, "zero", axis=2, tiled=True)
    part_router = (router_weight * router_gain[:, None]).astype(jnp.bfloat16)
    row_router = lax.all_gather(part_router, "zero", axis=0, tiled=True)
    serve_router = lax.all_gather(row_router, "bank", axis=1, tiled=True)
    return (final_down, scale_down, serve_router)


def solution(mesh):
    placed = (P("bank", None, "zero"), P("zero", "bank"), P("zero"))
    return jax.shard_map(
        per_device,
        mesh=mesh,
        in_specs=placed,
        out_specs=(P("bank", None, None), P("bank", None), P()),
        check_vma=False,
    )
```

profile of v0, /device:TPU:0, one launch (start us, length us, event | category | flops | bytes accessed | tf_op | source)
XLA Modules:
  0.0 634.6 jit_solution(17249483322936477532)
XLA Ops:
  7.2 0.0 all-gather.2.cloned.1.call-start
  7.2 7.1 %abs_reduce_fusion = f32[8,1024]{1,0:T(8,128)S(1)} fusion(f32[8,1024,512]{2,1,0:T(8,128)} %param.3), kind=kLoop, calls=%fused_computation.1 | loop fusion | flops 8380416 | bytes 16809984 | tf_op jit(solution)/shard_map/reduce_max | solution.py:8
  14.3 20.8 %pmax.7 = f32[8,1024]{1,0:T(8,128)S(1)} all-reduce(f32[8,1024]{1,0:T(8,128)S(1)} %abs_reduce_fusion), channel_id=1, replica_groups=mesh['bank'=8,'zero'=4] {'zero'}, use_global_device_ids=true, to_apply=%region_1.0 | all-reduce | flops 8192 | bytes 65536 | tf_op jit(solution)/shard_map/pmax | solution.py:8
  35.1 0.0 copy-start
  35.1 0.0 copy-start.1
  35.2 0.0 copy-start.2
  35.2 9.2 %divide_convert_fusion = bf16[8,1024,512]{2,1,0:T(8,128)(2,1)} fusion(f32[8,1024,512]{2,1,0:T(8,128)} %param.3, f32[8,1024]{1,0:T(8,128)S(1)} %pmax.7), kind=kLoop, calls=%fused_computation | loop fusion | flops 8388608 | bytes 25198592 | tf_op jit(solution)/shard_map/convert_element_type | solution.py:9
  44.3 0.0 all-gather.2.cloned.1.call-update
  44.4 0.0 copy-done
  44.4 0.0 copy-done.1
  44.4 0.0 copy-done.2
  44.4 13.1 %all_gather.10 = bf16[2048,8]{0,1:T(8,128)(2,1)S(1)} all-gather(bf16[512,8]{0,1:T(8,128)(2,1)S(1)} %multiply_convert_fusion), channel_id=1, replica_groups=mesh['bank'=8,'zero'=4] {'zero'}, dimensions={0}, use_global_device_ids=true | all-gather | bytes 40960 | tf_op jit(solution)/shard_map/all_gather | solution.py:12
  57.5 9.3 %all_gather.11 = bf16[2048,64]{0,1:T(8,128)(2,1)S(1)} all-gather(bf16[2048,8]{0,1:T(8,128)(2,1)S(1)} %all_gather.10), channel_id=1, replica_groups=mesh['bank'=8,'zero'=4] {'bank'}, dimensions={1}, use_global_device_ids=true | all-gather | bytes 294912 | tf_op jit(solution)/shard_map/all_gather | solution.py:13
  66.8 537.3 %all-gather.2.cloned.1.call-done = bf16[8,1024,2048]{2,1,0:T(8,128)(2,1)} async-done(((bf16[8,1024,512]{2,1,0:T(8,128)(2,1)}), bf16[8,1024,2048]{2,1,0:T(8,128)(2,1)}) %all-gather.2.cloned.1.call-update) | async-done | bytes 33554448 | tf_op jit(solution)/shard_map/all_gather | solution.py:10
  604.1 22.9 %copy.8 = bf16[8,1024,2048]{2,1,0:T(8,128)(2,1)} copy(bf16[8,1024,2048]{2,1,0:T(8,128)(2,1)} %all-gather.2.cloned.1.call-done) | data formatting | bytes 67108864
  627.0 0.7 copy.9
  (1 shorter events, 0.0 us)
Async XLA Ops:
  7.2 597.0 %all-gather.2.cloned.1.call-start = ((), (), s32[]{:S(2)}) async-start(), calls=%async_computation | async-start | bytes 41943040 | tf_op jit(solution)/shard_map/all_gather | solution.py:10
  35.1 9.2 %copy-start = (f32[8,1024]{1,0:T(8,128)}, f32[8,1024]{1,0:T(8,128)S(1)}, u32[]{:S(2)}) copy-start(f32[8,1024]{1,0:T(8,128)S(1)} %pmax.7) | copy-start | bytes 98308
  35.1 9.2 %copy-start.1 = (f32[512,8]{0,1:T(8,128)S(1)}, f32[512,8]{0,1:T(8,128)}, u32[]{:S(2)}) copy-start(f32[512,8]{0,1:T(8,128)} %param.4) | copy-start | bytes 49156
  35.2 9.2 %copy-start.2 = (f32[512]{0:T(512)S(1)}, f32[512]{0:T(512)}, u32[]{:S(2)}) copy-start(f32[512]{0:T(512)} %param.5) | copy-start | bytes 6148
Sparse Core Ops, SparseCore 0:
  44.5 559.6 all-gather.1
where the time goes:
time: 635 us
  waiting for transfers between devices  537 us (85%)
  blocking collectives  43.2 us (7%)
  local copies, waits for them, and re-layouts  23.6 us (4%)
  other arithmetic  16.3 us (3%)
  between operations  14.1 us (2%)
    all_gather x1, waiting for transfers between devices, per_device(): final_down = lax.all_gather(narrow_down, 'zero', axis=2, tiled=True)  537 us
    unnamed x8, local copies, waits for them, and re-layouts  23.6 us
    pmax x1, blocking collectives, per_device(): scale_down = lax.pmax(jnp.max(jnp.abs(master_down), axis=2), 'zero')  20.8 us
    all_gather x1, blocking collectives, per_device(): row_router = lax.all_gather(part_router, 'zero', axis=0, tiled=True)  13.1 us
  transfers between devices with their start and end apart: 1, of which 1 were waited for; matrix products, arithmetic and copies ran while one was open for 0% of the time, Pallas kernels for 0%

commit v1 on v0

--- a/solution.py
+++ b/solution.py
@@ -7,7 +7,8 @@
 def per_device(master_down, router_weight, router_gain):
     scale_down = lax.pmax(jnp.max(jnp.abs(master_down), axis=2), "zero")
     narrow_down = (master_down / jnp.expand_dims(scale_down, 2)).astype(jnp.bfloat16)
-    final_down = lax.all_gather(narrow_down, "zero", axis=2, tiled=True)
+    copies = jnp.concatenate([narrow_down] * lax.axis_size("zero"), axis=2)
+    final_down = lax.all_to_all(copies, "zero", 2, 2, tiled=True)
     part_router = (router_weight * router_gain[:, None]).astype(jnp.bfloat16)
     row_router = lax.all_gather(part_router, "zero", axis=0, tiled=True)
     serve_router = lax.all_gather(row_router, "bank", axis=1, tiled=True)

time: 635 us -> 883 us (1.39)
  blocking collectives: 43.2 us -> 754 us
  waiting for transfers between devices: 537 us -> 0.01 us
  local copies, waits for them, and re-layouts: 23.6 us -> 64.3 us
  other arithmetic: 16.3 us -> 52.4 us
  between operations: 14.1 us -> 0.7 us
  starting transfers between devices: 0.04 us -> 9.73 us
    all_gather x1, blocking collectives: 13.1 us -> 724 us  [per_device(): row_router = lax.all_gather(part_router, 'zero', axis=0, tiled=True)]
    all_gather x1 -> x0, waiting for transfers between devices: 537 us -> none  [per_device(): final_down = lax.all_gather(narrow_down, 'zero', axis=2, tiled=True)]
    unnamed x8 -> x9, local copies, waits for them, and re-layouts: 23.6 us -> 64.3 us
    concatenate x0 -> x1, other arithmetic: none -> 36 us  [per_device(): copies = jnp.concatenate([narrow_down] * lax.axis_size('zero'), axis=2)]
    all_to_all x0 -> x1, starting transfers between devices: none -> 9.73 us  [per_device(): final_down = lax.all_to_all(copies, 'zero', 2, 2, tiled=True)]
  transfers between devices with their start and end apart: 1 -> 1, of which waited for: 1 -> 0; matrix products, arithmetic and copies ran while one was open for 0% -> 0% of each run, Pallas kernels for 0% -> 0%
where the time goes in v1:
time: 883 us; the launch traced here: 881 us
  blocking collectives  754 us (85%)
  local copies, waits for them, and re-layouts  64.3 us (7%)
  other arithmetic  52.4 us (6%)
  starting transfers between devices  9.73 us (1%)
    all_gather x1, blocking collectives, per_device(): row_router = lax.all_gather(part_router, 'zero', axis=0, tiled=True)  724 us
    unnamed x9, local copies, waits for them, and re-layouts  64.3 us
    concatenate x1, other arithmetic, per_device(): copies = jnp.concatenate([narrow_down] * lax.axis_size('zero'), axis=2)  36 us
    pmax x1, blocking collectives, per_device(): scale_down = lax.pmax(jnp.max(jnp.abs(master_down), axis=2), 'zero')  20.8 us
  transfers between devices with their start and end apart: 1, of which 0 were waited for; matrix products, arithmetic and copies ran while one was open for 0% of the time, Pallas kernels for 0%

profile of v1, /device:TPU:0, one launch (start us, length us, event | category | flops | bytes accessed | tf_op | source)
XLA Modules:
  0.0 881.4 jit_solution(12545415169672977733)
XLA Ops:
  0.6 7.1 abs_reduce_fusion
  7.7 16.9 %copy.6 = f32[8,1024,512]{1,0,2:T(8,128)} copy(f32[8,1024,512]{2,1,0:T(8,128)} %param.3) | data formatting | bytes 33554432 | tf_op args[0]
  24.6 20.8 %pmax.7 = f32[8,1024]{1,0:T(8,128)S(1)} all-reduce(f32[8,1024]{1,0:T(8,128)S(1)} %abs_reduce_fusion), channel_id=1, replica_groups=mesh['bank'=8,'zero'=4] {'zero'}, use_global_device_ids=true, to_apply=%region_1.0 | all-reduce | flops 8192 | bytes 65536 | tf_op jit(solution)/shard_map/pmax | solution.py:8
  45.5 0.0 copy-start
  45.5 9.2 %divide_convert_fusion = bf16[8,1024,512]{1,0,2:T(8,128)(2,1)} fusion(f32[8,1024,512]{1,0,2:T(8,128)} %copy.6, f32[8,1024]{1,0:T(8,128)S(1)} %pmax.7), kind=kLoop, calls=%fused_computation.1 | loop fusion | flops 8388608 | bytes 25198592 | tf_op jit(solution)/shard_map/convert_element_type | solution.py:9
  54.7 36.0 %pad_maximum_fusion = bf16[8,1024,2048]{1,0,2:T(8,128)(2,1)} fusion(bf16[8,1024,512]{1,0,2:T(8,128)(2,1)} %divide_convert_fusion), kind=kLoop, calls=%fused_computation | loop fusion | flops 50331648 | bytes 41943040 | tf_op jit(solution)/shard_map/concatenate | solution.py:10
  90.7 0.0 copy-done
  90.7 0.0 copy-start.1
  90.8 0.0 copy-start.2
  90.8 9.7 %all-to-all-start = ((bf16[8,1024,2048]{1,0,2:T(8,128)(2,1)}), bf16[8,1024,2048]{1,0,2:T(8,128)(2,1)}, u32[]{:S(2)}, u32[]{:S(2)}) async-start(bf16[8,1024,2048]{1,0,2:T(8,128)(2,1)} %pad_maximum_fusion), calls=%async_computation | async-start | bytes 67108864 | tf_op jit(solution)/shard_map/all_to_all | solution.py:11
  100.5 0.0 copy-done.1
  100.5 0.0 copy-done.2
  100.5 724.2 %all_gather.6 = bf16[2048,8]{0,1:T(8,128)(2,1)S(1)} all-gather(bf16[512,8]{0,1:T(8,128)(2,1)S(1)} %multiply_convert_fusion), channel_id=1, replica_groups=mesh['bank'=8,'zero'=4] {'zero'}, dimensions={0}, use_global_device_ids=true | all-gather | bytes 40960 | tf_op jit(solution)/shard_map/all_gather | solution.py:13
  824.7 9.3 %all_gather.7 = bf16[2048,64]{0,1:T(8,128)(2,1)S(1)} all-gather(bf16[2048,8]{0,1:T(8,128)(2,1)S(1)} %all_gather.6), channel_id=1, replica_groups=mesh['bank'=8,'zero'=4] {'bank'}, dimensions={1}, use_global_device_ids=true | all-gather | bytes 294912 | tf_op jit(solution)/shard_map/all_gather | solution.py:14
  834.0 0.0 all-to-all-done
  834.0 46.6 %copy.7 = bf16[8,1024,2048]{2,1,0:T(8,128)(2,1)} copy(bf16[8,1024,2048]{1,0,2:T(8,128)(2,1)} %all-to-all-done) | data formatting | bytes 67108864
  880.7 0.7 copy.9
  (1 shorter events, 0.0 us)
Async XLA Ops:
  45.5 45.3 %copy-start = (f32[8,1024]{1,0:T(8,128)}, f32[8,1024]{1,0:T(8,128)S(1)}, u32[]{:S(2)}) copy-start(f32[8,1024]{1,0:T(8,128)S(1)} %pmax.7) | copy-start | bytes 98308
  90.7 9.8 %copy-start.1 = (f32[512,8]{0,1:T(8,128)S(1)}, f32[512,8]{0,1:T(8,128)}, u32[]{:S(2)}) copy-start(f32[512,8]{0,1:T(8,128)} %param.4) | copy-start | bytes 49156
  90.8 9.8 %copy-start.2 = (f32[512]{0:T(512)S(1)}, f32[512]{0:T(512)}, u32[]{:S(2)}) copy-start(f32[512]{0:T(512)} %param.5) | copy-start | bytes 6148
  90.8 743.3 %all-to-all-start = ((bf16[8,1024,2048]{1,0,2:T(8,128)(2,1)}), bf16[8,1024,2048]{1,0,2:T(8,128)(2,1)}, u32[]{:S(2)}, u32[]{:S(2)}) async-start(bf16[8,1024,2048]{1,0,2:T(8,128)(2,1)} %pad_maximum_fusion), calls=%async_computation | async-start | bytes 67108864 | tf_op jit(solution)/shard_map/all_to_all | solution.py:11
